TPU v7x, 32 devices: a whole 2x2x4 slice. The times are simulated.
32 devices in a mesh: grid: 8 (over y, x, core), band: 4 (over z).
Axes of the slice: x: 2, y: 2, z: 4, core: 2. Of those that a mesh axis runs over, the one named last changes fastest.
Arguments:
- start: float32 [1, 4, 1, 64, 32768], P(None, None, None, 'band', 'grid'), may hold values from -6 to 6
- energies: float32 [4, 64, 32768], P(None, 'band', 'grid'), may hold values from -4 to 4
- sites: int32 [3, 1], replicated, may hold values from 0 to 31
- potential: float32 [32, 32, 32], replicated, may hold values from -4 to 400
Outputs:
- alphas: float32 [1, 1, 4], replicated
- betas: float32 [1, 1, 4], replicated
- lanczos: float32 [1, 4, 1, 64, 32768], P(None, None, None, 'band', 'grid')
All inputs are finite; a program needn't handle non-finite values.
Results may differ from a plain program's by a relative error of at most 0.0003.
Values sent between devices are 32-bit elements; how exact they have to be, the bound alone decides.
A program may use at most 64 MiB of HBM per device.

v0:
```python
import math
import jax
import jax.numpy as jnp
from jax import lax
from jax.sharding import PartitionSpec as P

ITERS = 4
precise_mode = lax.Precision.HIGHEST


def cas_table(grid_size):
    cells = jnp.arange(grid_size, dtype=jnp.int32)
    phase = cells[:, None] * cells[None, :] % grid_size
    angle = phase.astype(jnp.float32) * (2.0 * math.pi / grid_size)
    return jnp.cos(angle) + jnp.sin(angle)


def shift_axis(field_part, offset, axis_number):
    length = field_part.shape[axis_number]
    doubled = jnp.concatenate([field_part, field_part], axis=axis_number)
    first_index = (length - offset) % length
    return lax.dynamic_slice_in_dim(doubled, first_index, length, axis_number)


def expand_coef(values):
    return values[:, None, :, None, None]


def body(start, energies, sites, potential):
    grid_size = potential.shape[0]
    volume = grid_size * grid_size * grid_size
    atom_count, core_count, pol_count, band_local, kpoint_local = start.shape
    plane_count = grid_size // lax.axis_size("grid")
    position = lax.axis_index("grid")
    chain_count = core_count * pol_count * band_local
    field_count = atom_count * chain_count
    total_count = (
        core_count * band_local * lax.axis_size("band") * kpoint_local * lax.axis_size("grid")
    )
    cas_grid = cas_table(grid_size)
    shifted = shift_axis(potential, sites[0, 0], 0)
    shifted = shift_axis(shifted, sites[1, 0], 1)
    shifted = shift_axis(shifted, sites[2, 0], 2)
    tables = [shifted]
    shifted_all = jnp.stack(tables, axis=-1)
    slab_table = lax.dynamic_slice_in_dim(shifted_all, position * plane_count, plane_count, 1)

    def moment(left, right):
        return jnp.sum(left * right, axis=(1, 3, 4)) / total_count

    start_sum = lax.psum(moment(start, start), ("grid", "band"))
    lanczos = start / expand_coef(jnp.sqrt(start_sum))
    previous = jnp.zeros_like(start)
    beta_prev = jnp.zeros((atom_count, pol_count), jnp.float32)
    alpha_list = []
    beta_list = []
    for iteration in range(ITERS):
        spread_fields = lanczos.reshape(atom_count, chain_count, plane_count, grid_size, grid_size)
        spread_over_z = jnp.einsum(
            "arpyz,wz->pywar", spread_fields, cas_grid, precision=precise_mode
        )
        spread_over_y = jnp.einsum(
            "pywar,uy->puwar", spread_over_z, cas_grid, precision=precise_mode
        )
        direct_spectrum = lax.all_to_all(
            spread_over_y.reshape(plane_count, grid_size, grid_size, field_count),
            "grid",
            split_axis=1,
            concat_axis=0,
            tiled=True,
        )
        field_shape = direct_spectrum.shape
        over_x = jnp.einsum("xvwf,tx->tvwf", direct_spectrum, cas_grid, precision=precise_mode)
        split_view = over_x.reshape(
            field_shape[0], field_shape[1], field_shape[2], atom_count, chain_count
        )
        scaled = split_view * slab_table[..., None]
        back_x = jnp.einsum("tvwar,xt->xvwar", scaled, cas_grid, precision=precise_mode)
        weighted = back_x.reshape(field_shape)
        direct_returned = lax.all_to_all(weighted, "grid", split_axis=0, concat_axis=1, tiled=True)
        fields = direct_returned.reshape(plane_count, grid_size, grid_size, atom_count, chain_count)
        over_z = jnp.einsum("pvwar,zw->pvzar", fields, cas_grid, precision=precise_mode)
        over_y = jnp.einsum("pvzar,yv->arpyz", over_z, cas_grid, precision=precise_mode)
        applied = energies[None, :, None] * lanczos - over_y.reshape(start.shape) / volume
        moments_all = lax.psum(
            (
                moment(lanczos, applied),
                moment(applied, applied),
                moment(lanczos, lanczos),
                moment(previous, previous),
                moment(previous, applied),
                moment(lanczos, previous),
            ),
            ("grid", "band"),
        )
        alpha_now = moments_all[0]
        square = (
            moments_all[1]
            + alpha_now * alpha_now * moments_all[2]
            + beta_prev * beta_prev * moments_all[3]
        )
        square = square - 2.0 * alpha_now * moments_all[0] - 2.0 * beta_prev * moments_all[4]
        square = square + 2.0 * alpha_now * beta_prev * moments_all[5]
        beta_now = jnp.sqrt(square)
        remainder = applied - expand_coef(alpha_now) * lanczos - expand_coef(beta_prev) * previous
        previous = lanczos
        lanczos = remainder / expand_coef(beta_now)
        beta_prev = beta_now
        alpha_list.append(alpha_now)
        beta_list.append(beta_now)
    return (jnp.stack(alpha_list, axis=2), jnp.stack(beta_list, axis=2), lanczos)


def solution(mesh):
    in_specs = (P(None, None, None, "band", "grid"), P(None, "band", "grid"), P(), P())
    out_specs = (P(), P(), P(None, None, None, "band", "grid"))
    return jax.shard_map(body, mesh=mesh, in_specs=in_specs, out_specs=out_specs, check_vma=False)
```

profile of v0, /device:TPU:0, one launch (start us, length us, event | category | flops | bytes accessed | tf_op | source)
XLA Modules:
  0.0 697.9 jit_solution(12863842465715470932)
XLA Ops:
  3.4 42.7 %psum.163 = f32[1,1]{1,0:T(1,128)} all-reduce(f32[1,1]{1,0:T(1,128)} %bitcast.1), channel_id=1, replica_groups=mesh['grid'=8,'band'=4] {'grid','band'}, use_global_device_ids=true, to_apply=%region_1.2 | all-reduce | flops 1 | bytes 8 | tf_op jit(solution)/shard_map/psum | solution.py:51
  48.0 2.7 reshape.300
  50.7 14.6 %fusion.60 = f32[4,32,32,64]{3,2,1,0:T(8,128)S(1)} fusion(f32[64,4,32,32]{3,2,1,0:T(8,128)} %reshape.300), kind=kOutput, calls=%fused_computation.48 | convolution fusion | flops 100678656 | bytes 2097152 | tf_op jit(solution)/shard_map/arpyz,wz->pywar/dot_general | solution.py:59
  65.4 3.0 fusion.40
  71.8 4.0 all-to-all-start
  79.0 12.1 %all-to-all-done = f32[8,1,32768]{2,1,0:T(1,128)S(1)} async-done(((f32[8,1,32768]{2,1,0:T(1,128)}), f32[8,1,32768]{2,1,0:T(1,128)S(1)}, u32[]{:S(2)}, u32[]{:S(2)}) %all-to-all-start) | async-done | bytes 1048608 | tf_op jit(solution)/shard_map/all_to_all | solution.py:65
  91.6 3.1 reduce.21
  95.8 3.0 fusion.28
  103.6 18.2 %all_to_all.132 = f32[8,1,32768]{2,1,0:T(1,128)S(1)} all-to-all(f32[8,1,32768]{2,1,0:T(1,128)S(1)} %reshape.323), channel_id=1, replica_groups=mesh['grid'=8,'band'=4] {'grid'}, dimensions={0} | all-to-all | bytes 2097152 | tf_op jit(solution)/shard_map/all_to_all | solution.py:80
  121.7 3.1 reduce.22
  127.9 3.0 multiply_bitcast_fusion.3
  130.9 4.5 copy.97
  135.5 3.7 div.203
  144.4 43.1 %all-reduce.3 = (f32[1,1]{1,0:T(1,128)}, f32[1,1]{1,0:T(1,128)}, f32[1,1]{1,0:T(1,128)}, f32[1,1]{1,0:T(1,128)}, f32[1,1]{1,0:T(1,128)}, /*index=5*/f32[1,1]{1,0:T(1,128)}) all-reduce(f32[1,1]{1,0:T(1,128)} %bitcast.31, f32[1,1]{1,0:T(1,128)} %bitcast.28, f32[1,1]{1,0:T(1,128)} %bitcast.32, ...), channel_id=1, replica_groups=mesh['grid'=8,'band'=4] {'grid','band'}, use_global_device_ids=true, to_apply=%region_5.6 | all-reduce | flops 6 | bytes 48 | tf_op jit(solution)/shard_map/psum | solution.py:85
  195.4 2.7 reshape.305
  198.1 14.6 %fusion.63 = f32[4,32,32,64]{3,2,1,0:T(8,128)S(1)} fusion(f32[64,4,32,32]{3,2,1,0:T(8,128)} %reshape.305), kind=kOutput, calls=%fused_computation.49 | convolution fusion | flops 100678656 | bytes 2097152 | tf_op jit(solution)/shard_map/arpyz,wz->pywar/dot_general | solution.py:59
  212.7 3.0 fusion.45
  218.3 3.3 reshape.325
  221.6 19.8 %all_to_all.133 = f32[8,1,32768]{2,1,0:T(1,128)} all-to-all(f32[8,1,32768]{2,1,0:T(1,128)} %reshape.325), channel_id=1, replica_groups=mesh['grid'=8,'band'=4] {'grid'}, dimensions={0} | all-to-all | bytes 2097152 | tf_op jit(solution)/shard_map/all_to_all | solution.py:65
  241.4 5.3 reduce.23
  246.7 3.4 reshape.326
  252.0 3.0 fusion.22
  259.7 3.3 reshape.327
  263.0 4.6 all-to-all-start.3
  268.3 14.8 %all-to-all-done.3 = f32[8,1,32768]{2,1,0:T(1,128)} async-done(((f32[8,1,32768]{2,1,0:T(1,128)}), f32[8,1,32768]{2,1,0:T(1,128)}, u32[]{:S(2)}, u32[]{:S(2)}) %all-to-all-start.3) | async-done | bytes 1048608 | tf_op jit(solution)/shard_map/all_to_all | solution.py:80
  283.1 5.3 reduce.24
  288.4 3.4 reshape.328
  295.6 4.4 multiply_bitcast_fusion.2
  299.9 5.6 copy.107
  305.5 4.3 div.220
  309.8 3.3 multiply_reduce_fusion.10
  316.3 41.5 %all-reduce.2 = (f32[1,1]{1,0:T(1,128)}, f32[1,1]{1,0:T(1,128)}, f32[1,1]{1,0:T(1,128)}, f32[1,1]{1,0:T(1,128)}, f32[1,1]{1,0:T(1,128)}) all-reduce(f32[1,1]{1,0:T(1,128)} %bitcast.57, f32[1,1]{1,0:T(1,128)} %bitcast.54, f32[1,1]{1,0:T(1,128)} %bitcast.58, f32[1,1]{1,0:T(1,128)} %bitcast.59, ...), channel_id=1, replica_groups=mesh['grid'=8,'band'=4] {'grid','band'}, use_global_device_ids=true, to_apply=%region_16.17 | all-reduce | flops 5 | bytes 40 | tf_op jit(solution)/shard_map/psum | solution.py:85
  364.9 2.7 reshape.310
  367.6 14.6 %fusion.66 = f32[4,32,32,64]{3,2,1,0:T(8,128)S(1)} fusion(f32[64,4,32,32]{3,2,1,0:T(8,128)} %reshape.310), kind=kOutput, calls=%fused_computation.50 | convolution fusion | flops 100678656 | bytes 2097152 | tf_op jit(solution)/shard_map/arpyz,wz->pywar/dot_general | solution.py:59
  382.2 3.0 fusion.50
  390.4 19.2 %all_to_all.134 = f32[8,1,32768]{2,1,0:T(1,128)} all-to-all(f32[8,1,32768]{2,1,0:T(1,128)S(1)} %reshape.329), channel_id=1, replica_groups=mesh['grid'=8,'band'=4] {'grid'}, dimensions={0} | all-to-all | bytes 2097152 | tf_op jit(solution)/shard_map/all_to_all | solution.py:65
  409.6 4.4 reduce.25
  418.0 3.0 fusion.16
  425.7 3.3 reshape.331
  429.0 4.6 all-to-all-start.5
  434.3 14.8 %all-to-all-done.5 = f32[8,1,32768]{2,1,0:T(1,128)} async-done(((f32[8,1,32768]{2,1,0:T(1,128)}), f32[8,1,32768]{2,1,0:T(1,128)}, u32[]{:S(2)}, u32[]{:S(2)}) %all-to-all-start.5) | async-done | bytes 1048608 | tf_op jit(solution)/shard_map/all_to_all | solution.py:80
  449.1 4.4 reduce.26
  459.4 4.4 multiply_bitcast_fusion.1
  463.7 5.6 copy.117
  469.3 4.4 div.237
  473.7 3.3 multiply_reduce_fusion.5
  480.2 42.5 %all-reduce.1 = (f32[1,1]{1,0:T(1,128)}, f32[1,1]{1,0:T(1,128)}, f32[1,1]{1,0:T(1,128)}, f32[1,1]{1,0:T(1,128)}, f32[1,1]{1,0:T(1,128)}) all-reduce(f32[1,1]{1,0:T(1,128)} %bitcast.83, f32[1,1]{1,0:T(1,128)} %bitcast.80, f32[1,1]{1,0:T(1,128)} %bitcast.84, f32[1,1]{1,0:T(1,128)} %bitcast.85, ...), channel_id=1, replica_groups=mesh['grid'=8,'band'=4] {'grid','band'}, use_global_device_ids=true, to_apply=%region_26.27 | all-reduce | flops 5 | bytes 40 | tf_op jit(solution)/shard_map/psum | solution.py:85
  529.5 2.7 reshape.315
  532.2 14.6 %fusion.69 = f32[4,32,32,64]{3,2,1,0:T(8,128)S(1)} fusion(f32[64,4,32,32]{3,2,1,0:T(8,128)} %reshape.315), kind=kOutput, calls=%fused_computation.51 | convolution fusion | flops 100678656 | bytes 2097152 | tf_op jit(solution)/shard_map/arpyz,wz->pywar/dot_general | solution.py:59
  546.8 3.0 fusion.55
  555.0 19.3 %all_to_all.135 = f32[8,1,32768]{2,1,0:T(1,128)} all-to-all(f32[8,1,32768]{2,1,0:T(1,128)S(1)} %reshape.333), channel_id=1, replica_groups=mesh['grid'=8,'band'=4] {'grid'}, dimensions={0} | all-to-all | bytes 2097152 | tf_op jit(solution)/shard_map/all_to_all | solution.py:65
  574.3 4.4 reduce.27
  582.6 3.0 fusion.10
  590.4 3.3 reshape.335
  593.7 4.5 all-to-all-start.7
  598.8 14.8 %all-to-all-done.7 = f32[8,1,32768]{2,1,0:T(1,128)} async-done(((f32[8,1,32768]{2,1,0:T(1,128)}), f32[8,1,32768]{2,1,0:T(1,128)}, u32[]{:S(2)}, u32[]{:S(2)}) %all-to-all-start.7) | async-done | bytes 1048608 | tf_op jit(solution)/shard_map/all_to_all | solution.py:80
  613.6 4.4 reduce.28
  623.9 4.4 multiply_bitcast_fusion
  628.2 5.6 copy.127
  633.8 4.4 div.254
  638.2 3.3 multiply_reduce_fusion
  644.8 41.3 %all-reduce = (f32[1,1]{1,0:T(1,128)}, f32[1,1]{1,0:T(1,128)}, f32[1,1]{1,0:T(1,128)}, f32[1,1]{1,0:T(1,128)}, f32[1,1]{1,0:T(1,128)}) all-reduce(f32[1,1]{1,0:T(1,128)} %bitcast.106, f32[1,1]{1,0:T(1,128)} %bitcast.111, f32[1,1]{1,0:T(1,128)} %bitcast.112, ...), channel_id=1, replica_groups=mesh['grid'=8,'band'=4] {'grid','band'}, use_global_device_ids=true, to_apply=%region_34.35 | all-reduce | flops 5 | bytes 40 | tf_op jit(solution)/shard_map/psum | solution.py:85
  691.4 3.1 divide_bitcast_fusion
  694.5 3.0 pad_maximum_fusion
  (58 shorter events, 77.6 us)
Async XLA Ops:
  69.6 6.2 copy-start.5
  69.6 8.8 %copy-start.4 = (f32[32,32,32]{2,1,0:T(8,128)S(1)}, f32[32,32,32]{2,1,0:T(8,128)}, u32[]{:S(2)}) copy-start(f32[32,32,32]{2,1,0:T(8,128)} %param.7) | copy-start | bytes 393220
  71.8 19.3 %all-to-all-start = ((f32[8,1,32768]{2,1,0:T(1,128)}), f32[8,1,32768]{2,1,0:T(1,128)S(1)}, u32[]{:S(2)}, u32[]{:S(2)}) async-start(f32[8,1,32768]{2,1,0:T(1,128)} %reshape.321), calls=%async_computation | async-start | bytes 2097152 | tf_op jit(solution)/shard_map/all_to_all | solution.py:65
  135.5 3.7 copy-start
  135.5 3.7 copy-start.1
  263.0 20.0 %all-to-all-start.3 = ((f32[8,1,32768]{2,1,0:T(1,128)}), f32[8,1,32768]{2,1,0:T(1,128)}, u32[]{:S(2)}, u32[]{:S(2)}) async-start(f32[8,1,32768]{2,1,0:T(1,128)} %reshape.327), calls=%async_computation.3 | async-start | bytes 2097152 | tf_op jit(solution)/shard_map/all_to_all | solution.py:80
  429.0 20.0 %all-to-all-start.5 = ((f32[8,1,32768]{2,1,0:T(1,128)}), f32[8,1,32768]{2,1,0:T(1,128)}, u32[]{:S(2)}, u32[]{:S(2)}) async-start(f32[8,1,32768]{2,1,0:T(1,128)} %reshape.331), calls=%async_computation.5 | async-start | bytes 2097152 | tf_op jit(solution)/shard_map/all_to_all | solution.py:80
  469.3 4.4 copy-start.2
  593.7 19.9 %all-to-all-start.7 = ((f32[8,1,32768]{2,1,0:T(1,128)}), f32[8,1,32768]{2,1,0:T(1,128)}, u32[]{:S(2)}, u32[]{:S(2)}) async-start(f32[8,1,32768]{2,1,0:T(1,128)} %reshape.335), calls=%async_computation.7 | async-start | bytes 2097152 | tf_op jit(solution)/shard_map/all_to_all | solution.py:80
  633.8 4.4 copy-start.3
where the time goes:
time: 709 us; the launch traced here: 698 us
  blocking collectives  287 us (40%)
  local copies, waits for them, and re-layouts  118 us (17%)
  matrix products  115 us (16%)
  other arithmetic  62.4 us (9%)
  waiting for transfers between devices  56.4 us (8%)
  between operations  40.5 us (6%)
  starting transfers between devices  17.7 us (2%)
    psum x4, blocking collectives, body(): lax.psum((moment(lanczos, applied), moment(applied, applied), moment(lanc...  168 us
    dot_general x4, matrix products, body(): jnp.einsum('arpyz,wz->pywar', spread_fields, cas_grid, precision=precise_...  58.4 us
    all_to_all x3, blocking collectives, body(): lax.all_to_all(spread_over_y.reshape(plane_count, grid_size, grid_size, f...  58.3 us
    all_to_all x3, waiting for transfers between devices, body(): lax.all_to_all(weighted, 'grid', split_axis=0, concat_axis=1, tiled=True)  44.3 us
    psum x1, blocking collectives, body(): start_sum = lax.psum(moment(start, start), ('grid', 'band'))  42.7 us
    unnamed x28, local copies, waits for them, and re-layouts  39.2 us
    div x8, local copies, waits for them, and re-layouts, body(): over_y.reshape(start.shape) / volume  38.1 us
    all_to_all x1, blocking collectives, body(): lax.all_to_all(weighted, 'grid', split_axis=0, concat_axis=1, tiled=True)  18.2 us
  transfers between devices with their start and end apart: 4, of which 4 were waited for; matrix products, arithmetic and copies ran while one was open for 0% of the time, Pallas kernels for 0%

commit v1 on v0

--- a/solution.py
+++ b/solution.py
@@ -6,6 +6,18 @@
 
 ITERS = 4
 precise_mode = lax.Precision.HIGHEST
+
+
+def split_up(value, dim, size):
+    shape = value.shape
+    blocks = value.reshape(*shape[:dim], size, shape[dim] // size, *shape[dim + 1 :])
+    return jnp.moveaxis(blocks, dim, 0)
+
+
+def joined_along(blocks, dim):
+    blocks = jnp.moveaxis(blocks, 0, dim)
+    dims = blocks.shape
+    return blocks.reshape(*dims[:dim], dims[dim] * dims[dim + 1], *dims[dim + 2 :])
 
 
 def cas_table(grid_size):
@@ -77,7 +89,14 @@
         scaled = split_view * slab_table[..., None]
         back_x = jnp.einsum("tvwar,xt->xvwar", scaled, cas_grid, precision=precise_mode)
         weighted = back_x.reshape(field_shape)
-        direct_returned = lax.all_to_all(weighted, "grid", split_axis=0, concat_axis=1, tiled=True)
+        size, place = (lax.axis_size("grid"), lax.axis_index("grid"))
+        blocks = split_up(weighted, 0, size)
+        outs = [blocks[place]]
+        for step in range(1, size):
+            sent = blocks[place ^ step]
+            outs.append(lax.ppermute(sent, "grid", [(i, i ^ step) for i in range(size)]))
+        blocks = jnp.stack(outs)[place ^ jnp.arange(size)]
+        direct_returned = joined_along(blocks, 1)
         fields = direct_returned.reshape(plane_count, grid_size, grid_size, atom_count, chain_count)
         over_z = jnp.einsum("pvwar,zw->pvzar", fields, cas_grid, precision=precise_mode)
         over_y = jnp.einsum("pvzar,yv->arpyz", over_z, cas_grid, precision=precise_mode)

time: 709 us -> 756 us (1.066)
  waiting for transfers between devices: 56.4 us -> 99.7 us
  local copies, waits for them, and re-layouts: 118 us -> 152 us
  blocking collectives: 287 us -> 269 us
  other arithmetic: 62.4 us -> 45.2 us
    ppermute x0 -> x28, waiting for transfers between devices: none -> 87.8 us  [body(): lax.ppermute(sent, 'grid', [(i, i ^ step) for i in range(size)])]
    all_to_all x3 -> x0, waiting for transfers between devices: 44.3 us -> none  [body(): lax.all_to_all(weighted, 'grid', split_axis=0, concat_axis=1, tiled=True)]
    another operation x4 -> x12, local copies, waits for them, and re-layouts: 10.8 us -> 48 us  [the longest x8 37.2 us: body(): blocks = jnp.stack(outs)[place ^ jnp.arange(size)]]
    all_to_all x1 -> x0, blocking collectives: 18.2 us -> none  [body(): lax.all_to_all(weighted, 'grid', split_axis=0, concat_axis=1, tiled=True)]
    all_to_all x4 -> x0, other arithmetic: 17.2 us -> none  [body(): lax.all_to_all(weighted, 'grid', split_axis=0, concat_axis=1, tiled=True)]
    ppermute x0 -> x28, starting transfers between devices: none -> 16.8 us  [body(): lax.ppermute(sent, 'grid', [(i, i ^ step) for i in range(size)])]
    unnamed x28 -> x66, local copies, waits for them, and re-layouts: 39.2 us -> 22.7 us
    all_to_all x3 -> x0, starting transfers between devices: 13.8 us -> none  [body(): lax.all_to_all(weighted, 'grid', split_axis=0, concat_axis=1, tiled=True)]
  transfers between devices with their start and end apart: 4 -> 29, of which waited for: 4 -> 13; matrix products, arithmetic and copies ran while one was open for 0% -> 0% of each run, Pallas kernels for 0% -> 0%
where the time goes in v1:
time: 756 us; the launch traced here: 743 us
  blocking collectives  269 us (36%)
  local copies, waits for them, and re-layouts  152 us (20%)
  matrix products  115 us (15%)
  waiting for transfers between devices  99.7 us (13%)
  other arithmetic  45.2 us (6%)
  between operations  41.2 us (5%)
  starting transfers between devices  20.7 us (3%)
    psum x4, blocking collectives, body(): lax.psum((moment(lanczos, applied), moment(applied, applied), moment(lanc...  168 us
    ppermute x28, waiting for transfers between devices, body(): lax.ppermute(sent, 'grid', [(i, i ^ step) for i in range(size)])  87.8 us
    dot_general x4, matrix products, body(): jnp.einsum('arpyz,wz->pywar', spread_fields, cas_grid, precision=precise_...  58.4 us
    all_to_all x3, blocking collectives, body(): lax.all_to_all(spread_over_y.reshape(plane_count, grid_size, grid_size, f...  58.3 us
    psum x1, blocking collectives, body(): start_sum = lax.psum(moment(start, start), ('grid', 'band'))  42.7 us
    div x8, local copies, waits for them, and re-layouts, body(): over_y.reshape(start.shape) / volume  38.1 us
    another operation x8, local copies, waits for them, and re-layouts, body(): blocks = jnp.stack(outs)[place ^ jnp.arange(size)]  37.2 us
    unnamed x66, local copies, waits for them, and re-layouts  22.7 us
  transfers between devices with their start and end apart: 29, of which 13 were waited for; matrix products, arithmetic and copies ran while one was open for 0% of the time, Pallas kernels for 0%

profile of v1, /device:TPU:0, one launch (start us, length us, event | category | flops | bytes accessed | tf_op | source)
XLA Modules:
  0.0 743.3 jit_solution(16079092427340174976)
XLA Ops:
  3.4 42.7 %psum.163 = f32[1,1]{1,0:T(1,128)} all-reduce(f32[1,1]{1,0:T(1,128)} %bitcast.1), channel_id=1, replica_groups=mesh['grid'=8,'band'=4] {'grid','band'}, use_global_device_ids=true, to_apply=%region_1.2 | all-reduce | flops 1 | bytes 8 | tf_op jit(solution)/shard_map/psum | solution.py:63
  50.8 14.6 %fusion.64 = f32[4,32,32,64]{3,2,1,0:T(8,128)S(1)} fusion(f32[64,4,32,32]{3,2,1,0:T(8,128)} %reshape.365), kind=kOutput, calls=%fused_computation.56 | convolution fusion | flops 100678656 | bytes 2097152 | tf_op jit(solution)/shard_map/arpyz,wz->pywar/dot_general | solution.py:71
  65.4 3.0 fusion.44
  71.8 3.9 all-to-all-start
  79.0 11.9 %all-to-all-done = f32[8,1,32768]{2,1,0:T(1,128)S(1)} async-done(((f32[8,1,32768]{2,1,0:T(1,128)}), f32[8,1,32768]{2,1,0:T(1,128)S(1)}, u32[]{:S(2)}, u32[]{:S(2)}) %all-to-all-start) | async-done | bytes 1048608 | tf_op jit(solution)/shard_map/all_to_all | solution.py:77
  91.4 3.1 reduce.21
  107.3 5.1 collective-permute-done.1
  112.8 4.1 collective-permute-done.2
  116.9 12.9 %collective-permute-done.4 = f32[4,4,32,64]{3,2,1,0:T(8,128)S(1)} collective-permute-done((f32[4,4,32,64]{3,2,1,0:T(8,128)S(1)}, f32[4,4,32,64]{3,2,1,0:T(8,128)S(1)}, u32[]{:S(2)}, u32[]{:S(2)}) %collective-permute-start.4) | collective-permute-done | bytes 131104 | tf_op jit(solution)/shard_map/ppermute | solution.py:97
  130.7 5.2 stack.134
  145.2 4.5 copy.97
  149.7 3.7 div.203
  158.7 43.0 %all-reduce.3 = (f32[1,1]{1,0:T(1,128)}, f32[1,1]{1,0:T(1,128)}, f32[1,1]{1,0:T(1,128)}, f32[1,1]{1,0:T(1,128)}, f32[1,1]{1,0:T(1,128)}, /*index=5*/f32[1,1]{1,0:T(1,128)}) all-reduce(f32[1,1]{1,0:T(1,128)} %bitcast.48, f32[1,1]{1,0:T(1,128)} %bitcast.45, f32[1,1]{1,0:T(1,128)} %bitcast.49, ...), channel_id=1, replica_groups=mesh['grid'=8,'band'=4] {'grid','band'}, use_global_device_ids=true, to_apply=%region_5.6 | all-reduce | flops 6 | bytes 48 | tf_op jit(solution)/shard_map/psum | solution.py:104
  212.3 14.6 %fusion.67 = f32[4,32,32,64]{3,2,1,0:T(8,128)S(1)} fusion(f32[64,4,32,32]{3,2,1,0:T(8,128)} %reshape.370), kind=kOutput, calls=%fused_computation.57 | convolution fusion | flops 100678656 | bytes 2097152 | tf_op jit(solution)/shard_map/arpyz,wz->pywar/dot_general | solution.py:71
  227.0 3.0 fusion.49
  232.6 3.3 reshape.425
  235.9 19.8 %all_to_all.72 = f32[8,1,32768]{2,1,0:T(1,128)} all-to-all(f32[8,1,32768]{2,1,0:T(1,128)} %reshape.425), channel_id=1, replica_groups=mesh['grid'=8,'band'=4] {'grid'}, dimensions={0} | all-to-all | bytes 2097152 | tf_op jit(solution)/shard_map/all_to_all | solution.py:77
  255.7 5.3 reduce.22
  261.0 3.4 reshape.426
  266.2 3.0 fusion.30
  277.9 5.1 collective-permute-done.8
  283.7 3.9 collective-permute-done.9
  287.6 12.9 %collective-permute-done.11 = f32[4,4,32,64]{3,2,1,0:T(8,128)S(1)} collective-permute-done((f32[4,4,32,64]{3,2,1,0:T(8,128)S(1)}, f32[4,4,32,64]{3,2,1,0:T(8,128)S(1)}, u32[]{:S(2)}, u32[]{:S(2)}) %collective-permute-start.11) | collective-permute-done | bytes 131104 | tf_op jit(solution)/shard_map/ppermute | solution.py:97
  301.3 6.9 stack.143
  308.2 3.3 copy.104
  311.5 3.6 gather_fusion.1
  318.9 4.4 multiply_bitcast_fusion.2
  323.2 5.6 copy.107
  328.9 4.3 div.220
  333.2 3.3 multiply_reduce_fusion.10
  339.6 41.5 %all-reduce.2 = (f32[1,1]{1,0:T(1,128)}, f32[1,1]{1,0:T(1,128)}, f32[1,1]{1,0:T(1,128)}, f32[1,1]{1,0:T(1,128)}, f32[1,1]{1,0:T(1,128)}) all-reduce(f32[1,1]{1,0:T(1,128)} %bitcast.89, f32[1,1]{1,0:T(1,128)} %bitcast.86, f32[1,1]{1,0:T(1,128)} %bitcast.90, f32[1,1]{1,0:T(1,128)} %bitcast.91, ...), channel_id=1, replica_groups=mesh['grid'=8,'band'=4] {'grid','band'}, use_global_device_ids=true, to_apply=%region_16.17 | all-reduce | flops 5 | bytes 40 | tf_op jit(solution)/shard_map/psum | solution.py:104
  390.8 14.6 %fusion.70 = f32[4,32,32,64]{3,2,1,0:T(8,128)S(1)} fusion(f32[64,4,32,32]{3,2,1,0:T(8,128)} %reshape.375), kind=kOutput, calls=%fused_computation.58 | convolution fusion | flops 100678656 | bytes 2097152 | tf_op jit(solution)/shard_map/arpyz,wz->pywar/dot_general | solution.py:71
  405.5 3.0 fusion.54
  413.6 19.2 %all_to_all.73 = f32[8,1,32768]{2,1,0:T(1,128)} all-to-all(f32[8,1,32768]{2,1,0:T(1,128)S(1)} %reshape.427), channel_id=1, replica_groups=mesh['grid'=8,'band'=4] {'grid'}, dimensions={0} | all-to-all | bytes 2097152 | tf_op jit(solution)/shard_map/all_to_all | solution.py:77
  432.9 4.4 reduce.23
  441.2 3.0 fusion.24
  452.9 5.1 collective-permute-done.15
  458.6 3.9 collective-permute-done.16
  462.5 12.9 %collective-permute-done.18 = f32[4,4,32,64]{3,2,1,0:T(8,128)S(1)} collective-permute-done((f32[4,4,32,64]{3,2,1,0:T(8,128)S(1)}, f32[4,4,32,64]{3,2,1,0:T(8,128)S(1)}, u32[]{:S(2)}, u32[]{:S(2)}) %collective-permute-start.18) | collective-permute-done | bytes 131104 | tf_op jit(solution)/shard_map/ppermute | solution.py:97
  476.3 6.8 stack.152
  483.0 3.3 copy.114
  486.3 3.6 gather_fusion.2
  493.7 4.4 multiply_bitcast_fusion.1
  498.0 5.6 copy.117
  503.7 4.4 div.237
  508.1 3.3 multiply_reduce_fusion.5
  514.5 42.4 %all-reduce.1 = (f32[1,1]{1,0:T(1,128)}, f32[1,1]{1,0:T(1,128)}, f32[1,1]{1,0:T(1,128)}, f32[1,1]{1,0:T(1,128)}, f32[1,1]{1,0:T(1,128)}) all-reduce(f32[1,1]{1,0:T(1,128)} %bitcast.129, f32[1,1]{1,0:T(1,128)} %bitcast.126, f32[1,1]{1,0:T(1,128)} %bitcast.130, ...), channel_id=1, replica_groups=mesh['grid'=8,'band'=4] {'grid','band'}, use_global_device_ids=true, to_apply=%region_26.27 | all-reduce | flops 5 | bytes 40 | tf_op jit(solution)/shard_map/psum | solution.py:104
  566.4 14.6 %fusion.73 = f32[4,32,32,64]{3,2,1,0:T(8,128)S(1)} fusion(f32[64,4,32,32]{3,2,1,0:T(8,128)} %reshape.380), kind=kOutput, calls=%fused_computation.59 | convolution fusion | flops 100678656 | bytes 2097152 | tf_op jit(solution)/shard_map/arpyz,wz->pywar/dot_general | solution.py:71
  589.2 19.3 %all_to_all.74 = f32[8,1,32768]{2,1,0:T(1,128)} all-to-all(f32[8,1,32768]{2,1,0:T(1,128)S(1)} %reshape.429), channel_id=1, replica_groups=mesh['grid'=8,'band'=4] {'grid'}, dimensions={0} | all-to-all | bytes 2097152 | tf_op jit(solution)/shard_map/all_to_all | solution.py:77
  608.5 4.4 reduce.24
  616.9 3.0 fusion.18
  628.5 5.1 collective-permute-done.22
  634.3 3.9 collective-permute-done.23
  638.2 12.9 %collective-permute-done.25 = f32[4,4,32,64]{3,2,1,0:T(8,128)S(1)} collective-permute-done((f32[4,4,32,64]{3,2,1,0:T(8,128)S(1)}, f32[4,4,32,64]{3,2,1,0:T(8,128)S(1)}, u32[]{:S(2)}, u32[]{:S(2)}) %collective-permute-start.25) | collective-permute-done | bytes 131104 | tf_op jit(solution)/shard_map/ppermute | solution.py:97
  652.0 6.7 stack.161
  658.6 3.3 copy.124
  661.9 3.6 gather_fusion.3
  669.3 4.4 multiply_bitcast_fusion
  673.7 5.6 copy.127
  679.3 4.4 div.254
  683.7 3.3 multiply_reduce_fusion
  690.2 41.2 %all-reduce = (f32[1,1]{1,0:T(1,128)}, f32[1,1]{1,0:T(1,128)}, f32[1,1]{1,0:T(1,128)}, f32[1,1]{1,0:T(1,128)}, f32[1,1]{1,0:T(1,128)}) all-reduce(f32[1,1]{1,0:T(1,128)} %bitcast.166, f32[1,1]{1,0:T(1,128)} %bitcast.171, f32[1,1]{1,0:T(1,128)} %bitcast.172, ...), channel_id=1, replica_groups=mesh['grid'=8,'band'=4] {'grid','band'}, use_global_device_ids=true, to_apply=%region_34.35 | all-reduce | flops 5 | bytes 40 | tf_op jit(solution)/shard_map/psum | solution.py:104
  736.7 3.1 divide_bitcast_fusion
  739.8 3.0 pad_maximum_fusion
  (156 shorter events, 115.4 us)
Async XLA Ops:
  69.6 6.1 copy-start.28
  69.6 8.8 %copy-start.4 = (f32[32,32,32]{2,1,0:T(8,128)S(1)}, f32[32,32,32]{2,1,0:T(8,128)}, u32[]{:S(2)}) copy-start(f32[32,32,32]{2,1,0:T(8,128)} %param.7) | copy-start | bytes 393220
  71.8 19.1 %all-to-all-start = ((f32[8,1,32768]{2,1,0:T(1,128)}), f32[8,1,32768]{2,1,0:T(1,128)S(1)}, u32[]{:S(2)}, u32[]{:S(2)}) async-start(f32[8,1,32768]{2,1,0:T(1,128)} %reshape.423), calls=%async_computation | async-start | bytes 2097152 | tf_op jit(solution)/shard_map/all_to_all | solution.py:77
  103.1 3.6 collective-permute-start
  103.1 9.2 %collective-permute-start.1 = (f32[4,4,32,64]{3,2,1,0:T(8,128)S(1)}, f32[4,4,32,64]{3,2,1,0:T(8,128)S(1)}, u32[]{:S(2)}, u32[]{:S(2)}) collective-permute-start(f32[4,4,32,64]{3,2,1,0:T(8,128)S(1)} %bitcast.416), channel_id=1, source_target_pairs={{0,8},{4,12},{8,0},{12,4},{16,24},{20,28},{24,16},{28,20},{1,9},{5... | collective-permute-start | bytes 393224 | tf_op jit(solution)/shard_map/ppermute | solution.py:97
  103.7 13.2 %collective-permute-start.2 = (f32[4,4,32,64]{3,2,1,0:T(8,128)S(1)}, f32[4,4,32,64]{3,2,1,0:T(8,128)S(1)}, u32[]{:S(2)}, u32[]{:S(2)}) collective-permute-start(f32[4,4,32,64]{3,2,1,0:T(8,128)S(1)} %bitcast.408), channel_id=1, source_target_pairs={{0,12},{4,8},{8,4},{12,0},{16,28},{20,24},{24,20},{28,16},{1,13},{... | collective-permute-start | bytes 393224 | tf_op jit(solution)/shard_map/ppermute | solution.py:97
  105.0 11.9 %collective-permute-start.3 = (f32[4,4,32,64]{3,2,1,0:T(8,128)S(1)}, f32[4,4,32,64]{3,2,1,0:T(8,128)S(1)}, u32[]{:S(2)}, u32[]{:S(2)}) collective-permute-start(f32[4,4,32,64]{3,2,1,0:T(8,128)S(1)} %bitcast.401), channel_id=1, source_target_pairs={{0,16},{4,20},{8,24},{12,28},{16,0},{20,4},{24,8},{28,12},{1,17},{... | collective-permute-start | bytes 393224 | tf_op jit(solution)/shard_map/ppermute | solution.py:97
  105.6 24.2 %collective-permute-start.4 = (f32[4,4,32,64]{3,2,1,0:T(8,128)S(1)}, f32[4,4,32,64]{3,2,1,0:T(8,128)S(1)}, u32[]{:S(2)}, u32[]{:S(2)}) collective-permute-start(f32[4,4,32,64]{3,2,1,0:T(8,128)S(1)} %bitcast.394), channel_id=1, source_target_pairs={{0,20},{4,16},{8,28},{12,24},{16,4},{20,0},{24,12},{28,8},{1,21},{... | collective-permute-start | bytes 393224 | tf_op jit(solution)/shard_map/ppermute | solution.py:97
  106.7 23.1 %collective-permute-start.5 = (f32[4,4,32,64]{3,2,1,0:T(8,128)S(1)}, f32[4,4,32,64]{3,2,1,0:T(8,128)S(1)}, u32[]{:S(2)}, u32[]{:S(2)}) collective-permute-start(f32[4,4,32,64]{3,2,1,0:T(8,128)S(1)} %bitcast.386), channel_id=1, source_target_pairs={{0,24},{4,28},{8,16},{12,20},{16,8},{20,12},{24,0},{28,4},{1,25},{... | collective-permute-start | bytes 393224 | tf_op jit(solution)/shard_map/ppermute | solution.py:97
  112.4 17.4 %collective-permute-start.6 = (f32[4,4,32,64]{3,2,1,0:T(8,128)S(1)}, f32[4,4,32,64]{3,2,1,0:T(8,128)S(1)}, u32[]{:S(2)}, u32[]{:S(2)}) collective-permute-start(f32[4,4,32,64]{3,2,1,0:T(8,128)S(1)} %bitcast.378), channel_id=1, source_target_pairs={{0,28},{4,24},{8,20},{12,16},{16,12},{20,8},{24,4},{28,0},{1,29},{... | collective-permute-start | bytes 393224 | tf_op jit(solution)/shard_map/ppermute | solution.py:97
  116.9 12.9 %copy-start.11 = (f32[4,4,32,64]{3,2,1,0:T(8,128)}, f32[4,4,32,64]{3,2,1,0:T(8,128)S(1)}, u32[]{:S(2)}) copy-start(f32[4,4,32,64]{3,2,1,0:T(8,128)S(1)} %collective-permute-done.2) | copy-start | bytes 393220
  116.9 12.9 %copy-start.15 = (f32[4,4,32,64]{3,2,1,0:T(8,128)}, f32[4,4,32,64]{3,2,1,0:T(8,128)S(1)}, u32[]{:S(2)}) copy-start(f32[4,4,32,64]{3,2,1,0:T(8,128)S(1)} %collective-permute-done.3) | copy-start | bytes 393220
  129.8 0.7 copy-start.19
  129.8 0.8 copy-start.23
  129.8 0.9 copy-start.27
  149.7 3.7 copy-start
  149.7 3.7 copy-start.1
  273.7 3.6 collective-permute-start.7
  273.8 9.2 %collective-permute-start.8 = (f32[4,4,32,64]{3,2,1,0:T(8,128)S(1)}, f32[4,4,32,64]{3,2,1,0:T(8,128)S(1)}, u32[]{:S(2)}, u32[]{:S(2)}) collective-permute-start(f32[4,4,32,64]{3,2,1,0:T(8,128)S(1)} %bitcast.417), channel_id=1, source_target_pairs={{0,8},{4,12},{8,0},{12,4},{16,24},{20,28},{24,16},{28,20},{1,9},{5... | collective-permute-start | bytes 393224 | tf_op jit(solution)/shard_map/ppermute | solution.py:97
  274.4 13.2 %collective-permute-start.9 = (f32[4,4,32,64]{3,2,1,0:T(8,128)S(1)}, f32[4,4,32,64]{3,2,1,0:T(8,128)S(1)}, u32[]{:S(2)}, u32[]{:S(2)}) collective-permute-start(f32[4,4,32,64]{3,2,1,0:T(8,128)S(1)} %bitcast.403), channel_id=1, source_target_pairs={{0,12},{4,8},{8,4},{12,0},{16,28},{20,24},{24,20},{28,16},{1,13},{... | collective-permute-start | bytes 393224 | tf_op jit(solution)/shard_map/ppermute | solution.py:97
  275.6 11.9 %collective-permute-start.10 = (f32[4,4,32,64]{3,2,1,0:T(8,128)S(1)}, f32[4,4,32,64]{3,2,1,0:T(8,128)S(1)}, u32[]{:S(2)}, u32[]{:S(2)}) collective-permute-start(f32[4,4,32,64]{3,2,1,0:T(8,128)S(1)} %bitcast.396), channel_id=1, source_target_pairs={{0,16},{4,20},{8,24},{12,28},{16,0},{20,4},{24,8},{28,12},{1,17},{... | collective-permute-start | bytes 393224 | tf_op jit(solution)/shard_map/ppermute | solution.py:97
  276.2 24.3 %collective-permute-start.11 = (f32[4,4,32,64]{3,2,1,0:T(8,128)S(1)}, f32[4,4,32,64]{3,2,1,0:T(8,128)S(1)}, u32[]{:S(2)}, u32[]{:S(2)}) collective-permute-start(f32[4,4,32,64]{3,2,1,0:T(8,128)S(1)} %bitcast.389), channel_id=1, source_target_pairs={{0,20},{4,16},{8,28},{12,24},{16,4},{20,0},{24,12},{28,8},{1,21},{... | collective-permute-start | bytes 393224 | tf_op jit(solution)/shard_map/ppermute | solution.py:97
  277.4 23.1 %copy-start.5 = (f32[4,4,32,64]{3,2,1,0:T(8,128)}, f32[4,4,32,64]{3,2,1,0:T(8,128)S(1)}, u32[]{:S(2)}) copy-start(f32[4,4,32,64]{3,2,1,0:T(8,128)S(1)} %collective-permute-done.7) | copy-start | bytes 393220
  277.4 23.1 %collective-permute-start.12 = (f32[4,4,32,64]{3,2,1,0:T(8,128)S(1)}, f32[4,4,32,64]{3,2,1,0:T(8,128)S(1)}, u32[]{:S(2)}, u32[]{:S(2)}) collective-permute-start(f32[4,4,32,64]{3,2,1,0:T(8,128)S(1)} %bitcast.381), channel_id=1, source_target_pairs={{0,24},{4,28},{8,16},{12,20},{16,8},{20,12},{24,0},{28,4},{1,25},{... | collective-permute-start | bytes 393224 | tf_op jit(solution)/shard_map/ppermute | solution.py:97
  283.0 17.4 %copy-start.6 = (f32[4,4,32,64]{3,2,1,0:T(8,128)}, f32[4,4,32,64]{3,2,1,0:T(8,128)S(1)}, u32[]{:S(2)}) copy-start(f32[4,4,32,64]{3,2,1,0:T(8,128)S(1)} %collective-permute-done.8) | copy-start | bytes 393220
  283.0 17.4 %collective-permute-start.13 = (f32[4,4,32,64]{3,2,1,0:T(8,128)S(1)}, f32[4,4,32,64]{3,2,1,0:T(8,128)S(1)}, u32[]{:S(2)}, u32[]{:S(2)}) collective-permute-start(f32[4,4,32,64]{3,2,1,0:T(8,128)S(1)} %bitcast.373), channel_id=1, source_target_pairs={{0,28},{4,24},{8,20},{12,16},{16,12},{20,8},{24,4},{28,0},{1,29},{... | collective-permute-start | bytes 393224 | tf_op jit(solution)/shard_map/ppermute | solution.py:97
  287.6 12.9 %copy-start.8 = (f32[4,4,32,64]{3,2,1,0:T(8,128)}, f32[4,4,32,64]{3,2,1,0:T(8,128)S(1)}, u32[]{:S(2)}) copy-start(f32[4,4,32,64]{3,2,1,0:T(8,128)S(1)} %collective-permute-done.9) | copy-start | bytes 393220
  287.6 12.9 %copy-start.12 = (f32[4,4,32,64]{3,2,1,0:T(8,128)}, f32[4,4,32,64]{3,2,1,0:T(8,128)S(1)}, u32[]{:S(2)}) copy-start(f32[4,4,32,64]{3,2,1,0:T(8,128)S(1)} %collective-permute-done.10) | copy-start | bytes 393220
  300.5 0.7 copy-start.16
  300.5 0.8 copy-start.20
  300.5 0.9 copy-start.24
  448.6 3.6 collective-permute-start.14
  448.7 9.2 %collective-permute-start.15 = (f32[4,4,32,64]{3,2,1,0:T(8,128)S(1)}, f32[4,4,32,64]{3,2,1,0:T(8,128)S(1)}, u32[]{:S(2)}, u32[]{:S(2)}) collective-permute-start(f32[4,4,32,64]{3,2,1,0:T(8,128)S(1)} %bitcast.418), channel_id=1, source_target_pairs={{0,8},{4,12},{8,0},{12,4},{16,24},{20,28},{24,16},{28,20},{1,9},{5... | collective-permute-start | bytes 393224 | tf_op jit(solution)/shard_map/ppermute | solution.py:97
  449.3 13.2 %collective-permute-start.16 = (f32[4,4,32,64]{3,2,1,0:T(8,128)S(1)}, f32[4,4,32,64]{3,2,1,0:T(8,128)S(1)}, u32[]{:S(2)}, u32[]{:S(2)}) collective-permute-start(f32[4,4,32,64]{3,2,1,0:T(8,128)S(1)} %bitcast.405), channel_id=1, source_target_pairs={{0,12},{4,8},{8,4},{12,0},{16,28},{20,24},{24,20},{28,16},{1,13},{... | collective-permute-start | bytes 393224 | tf_op jit(solution)/shard_map/ppermute | solution.py:97
  450.6 11.9 %collective-permute-start.17 = (f32[4,4,32,64]{3,2,1,0:T(8,128)S(1)}, f32[4,4,32,64]{3,2,1,0:T(8,128)S(1)}, u32[]{:S(2)}, u32[]{:S(2)}) collective-permute-start(f32[4,4,32,64]{3,2,1,0:T(8,128)S(1)} %bitcast.398), channel_id=1, source_target_pairs={{0,16},{4,20},{8,24},{12,28},{16,0},{20,4},{24,8},{28,12},{1,17},{... | collective-permute-start | bytes 393224 | tf_op jit(solution)/shard_map/ppermute | solution.py:97
  451.1 24.2 %collective-permute-start.18 = (f32[4,4,32,64]{3,2,1,0:T(8,128)S(1)}, f32[4,4,32,64]{3,2,1,0:T(8,128)S(1)}, u32[]{:S(2)}, u32[]{:S(2)}) collective-permute-start(f32[4,4,32,64]{3,2,1,0:T(8,128)S(1)} %bitcast.391), channel_id=1, source_target_pairs={{0,20},{4,16},{8,28},{12,24},{16,4},{20,0},{24,12},{28,8},{1,21},{... | collective-permute-start | bytes 393224 | tf_op jit(solution)/shard_map/ppermute | solution.py:97
  452.3 23.1 %collective-permute-start.19 = (f32[4,4,32,64]{3,2,1,0:T(8,128)S(1)}, f32[4,4,32,64]{3,2,1,0:T(8,128)S(1)}, u32[]{:S(2)}, u32[]{:S(2)}) collective-permute-start(f32[4,4,32,64]{3,2,1,0:T(8,128)S(1)} %bitcast.383), channel_id=1, source_target_pairs={{0,24},{4,28},{8,16},{12,20},{16,8},{20,12},{24,0},{28,4},{1,25},{... | collective-permute-start | bytes 393224 | tf_op jit(solution)/shard_map/ppermute | solution.py:97
  458.0 17.4 %collective-permute-start.20 = (f32[4,4,32,64]{3,2,1,0:T(8,128)S(1)}, f32[4,4,32,64]{3,2,1,0:T(8,128)S(1)}, u32[]{:S(2)}, u32[]{:S(2)}) collective-permute-start(f32[4,4,32,64]{3,2,1,0:T(8,128)S(1)} %bitcast.375), channel_id=1, source_target_pairs={{0,28},{4,24},{8,20},{12,16},{16,12},{20,8},{24,4},{28,0},{1,29},{... | collective-permute-start | bytes 393224 | tf_op jit(solution)/shard_map/ppermute | solution.py:97
  462.5 12.9 %copy-start.9 = (f32[4,4,32,64]{3,2,1,0:T(8,128)}, f32[4,4,32,64]{3,2,1,0:T(8,128)S(1)}, u32[]{:S(2)}) copy-start(f32[4,4,32,64]{3,2,1,0:T(8,128)S(1)} %collective-permute-done.16) | copy-start | bytes 393220
  462.5 12.9 %copy-start.13 = (f32[4,4,32,64]{3,2,1,0:T(8,128)}, f32[4,4,32,64]{3,2,1,0:T(8,128)S(1)}, u32[]{:S(2)}) copy-start(f32[4,4,32,64]{3,2,1,0:T(8,128)S(1)} %collective-permute-done.17) | copy-start | bytes 393220
  475.4 0.7 copy-start.17
  475.4 0.8 copy-start.21
  475.4 0.9 copy-start.25
  503.7 4.4 copy-start.2
  624.3 3.6 collective-permute-start.21
  624.4 9.2 %collective-permute-start.22 = (f32[4,4,32,64]{3,2,1,0:T(8,128)S(1)}, f32[4,4,32,64]{3,2,1,0:T(8,128)S(1)}, u32[]{:S(2)}, u32[]{:S(2)}) collective-permute-start(f32[4,4,32,64]{3,2,1,0:T(8,128)S(1)} %bitcast.410), channel_id=1, source_target_pairs={{0,8},{4,12},{8,0},{12,4},{16,24},{20,28},{24,16},{28,20},{1,9},{5... | collective-permute-start | bytes 393224 | tf_op jit(solution)/shard_map/ppermute | solution.py:97
  625.0 13.2 %collective-permute-start.23 = (f32[4,4,32,64]{3,2,1,0:T(8,128)S(1)}, f32[4,4,32,64]{3,2,1,0:T(8,128)S(1)}, u32[]{:S(2)}, u32[]{:S(2)}) collective-permute-start(f32[4,4,32,64]{3,2,1,0:T(8,128)S(1)} %bitcast.388), channel_id=1, source_target_pairs={{0,12},{4,8},{8,4},{12,0},{16,28},{20,24},{24,20},{28,16},{1,13},{... | collective-permute-start | bytes 393224 | tf_op jit(solution)/shard_map/ppermute | solution.py:97
  626.3 11.9 %collective-permute-start.24 = (f32[4,4,32,64]{3,2,1,0:T(8,128)S(1)}, f32[4,4,32,64]{3,2,1,0:T(8,128)S(1)}, u32[]{:S(2)}, u32[]{:S(2)}) collective-permute-start(f32[4,4,32,64]{3,2,1,0:T(8,128)S(1)} %bitcast.380), channel_id=1, source_target_pairs={{0,16},{4,20},{8,24},{12,28},{16,0},{20,4},{24,8},{28,12},{1,17},{... | collective-permute-start | bytes 393224 | tf_op jit(solution)/shard_map/ppermute | solution.py:97
  626.8 24.2 %collective-permute-start.25 = (f32[4,4,32,64]{3,2,1,0:T(8,128)S(1)}, f32[4,4,32,64]{3,2,1,0:T(8,128)S(1)}, u32[]{:S(2)}, u32[]{:S(2)}) collective-permute-start(f32[4,4,32,64]{3,2,1,0:T(8,128)S(1)} %bitcast.372), channel_id=1, source_target_pairs={{0,20},{4,16},{8,28},{12,24},{16,4},{20,0},{24,12},{28,8},{1,21},{... | collective-permute-start | bytes 393224 | tf_op jit(solution)/shard_map/ppermute | solution.py:97
  628.0 23.1 %collective-permute-start.26 = (f32[4,4,32,64]{3,2,1,0:T(8,128)S(1)}, f32[4,4,32,64]{3,2,1,0:T(8,128)S(1)}, u32[]{:S(2)}, u32[]{:S(2)}) collective-permute-start(f32[4,4,32,64]{3,2,1,0:T(8,128)S(1)} %bitcast.371), channel_id=1, source_target_pairs={{0,24},{4,28},{8,16},{12,20},{16,8},{20,12},{24,0},{28,4},{1,25},{... | collective-permute-start | bytes 393224 | tf_op jit(solution)/shard_map/ppermute | solution.py:97
  633.7 17.4 %copy-start.7 = (f32[4,4,32,64]{3,2,1,0:T(8,128)}, f32[4,4,32,64]{3,2,1,0:T(8,128)S(1)}, u32[]{:S(2)}) copy-start(f32[4,4,32,64]{3,2,1,0:T(8,128)S(1)} %collective-permute-done.22) | copy-start | bytes 393220
  633.7 17.4 %collective-permute-start.27 = (f32[4,4,32,64]{3,2,1,0:T(8,128)S(1)}, f32[4,4,32,64]{3,2,1,0:T(8,128)S(1)}, u32[]{:S(2)}, u32[]{:S(2)}) collective-permute-start(f32[4,4,32,64]{3,2,1,0:T(8,128)S(1)} %bitcast.370), channel_id=1, source_target_pairs={{0,28},{4,24},{8,20},{12,16},{16,12},{20,8},{24,4},{28,0},{1,29},{... | collective-permute-start | bytes 393224 | tf_op jit(solution)/shard_map/ppermute | solution.py:97
  638.2 12.9 %copy-start.10 = (f32[4,4,32,64]{3,2,1,0:T(8,128)}, f32[4,4,32,64]{3,2,1,0:T(8,128)S(1)}, u32[]{:S(2)}) copy-start(f32[4,4,32,64]{3,2,1,0:T(8,128)S(1)} %collective-permute-done.23) | copy-start | bytes 393220
  638.2 12.9 %copy-start.14 = (f32[4,4,32,64]{3,2,1,0:T(8,128)}, f32[4,4,32,64]{3,2,1,0:T(8,128)S(1)}, u32[]{:S(2)}) copy-start(f32[4,4,32,64]{3,2,1,0:T(8,128)S(1)} %collective-permute-done.24) | copy-start | bytes 393220
  651.1 0.7 copy-start.18
  651.1 0.8 copy-start.22
  651.1 0.9 copy-start.26
  679.3 4.4 copy-start.3
